TPU v7x, 256 devices: a whole 4x4x8 slice. The times are simulated.
256 devices in a mesh: tok: 16 (over z, core), vocab: 16 (over y, x).
Axes of the slice: x: 4, y: 4, z: 8, core: 2. Of those that a mesh axis runs over, the one named last changes fastest.
Arguments:
- latent_vectors: float32 [1536, 3584], P('tok'), may hold values from -400 to 400
- unembedding_matrix: float32 [3584, 152064], P(None, ('tok', 'vocab')), may hold values from -0.09375 to 0.09375
- drawn_symbols: int32 [1536], P('tok'), may hold values from 0 to 152063
- piece_extents: int32 [16, 4], P('tok'), may hold values from 1 to 48, 96 in all within a row
- piece_episode_lookup: int32 [16, 4], P('tok'), may hold values from 0 to 1023
- episode_heats: float32 [1024], replicated, may hold values from 0.6 to 1.5
Outputs:
- seg_logprob: float32 [64], P('tok')
Inputs may be any that keep to these rules, and one draw needn't show every extreme that they name: `piece_extents`: each row of lengths sums to 96.
All inputs are finite; a program needn't handle non-finite values.
Results may differ from a plain program's by a relative error of at most 0.0003.
Values sent between devices are 32-bit elements; how exact they have to be, the bound alone decides.
A program may use at most 128 MiB of HBM per device.

v0:
```python
import jax
import jax.numpy as jnp
from jax import lax
from jax.sharding import Mesh
from jax.sharding import PartitionSpec as P

TOK = ("tok_0", "tok_1")
VOCAB = ("vocab_0", "vocab_1")
TOK_VOCAB = ("tok_0", "tok_1", "vocab_0", "vocab_1")


def collected_together(x, axis):
    leaves = jax.tree.leaves(x)
    order = sorted(range(len(leaves)), key=lambda k: -leaves[k].size)
    width = (1, *leaves[order[0]].shape)[-1]
    lines = [
        jnp.pad(leaves[k].reshape(-1), (0, -leaves[k].size % width)).reshape(-1, width)
        for k in order
    ]
    both, at, found = (lax.all_gather(jnp.concatenate(lines), axis), 0, {})
    for k, line in zip(order, lines):
        piece = both[:, at : at + len(line)].reshape(len(both), -1)
        found[k] = piece[:, : leaves[k].size].reshape(-1, *leaves[k].shape)
        at += len(line)
    numbers = iter(range(len(leaves)))
    return jax.tree.map(lambda _: found[next(numbers)], x)


def merged_by_axis(x, axes, combine):
    for axis in axes:
        pieces = collected_together(x, axis)
        x = jax.tree.map(lambda part: part[0], pieces)
        for k in range(1, lax.axis_size(axis)):
            x = combine(x, jax.tree.map(lambda part: part[k], pieces))
    return x


def combine_pairs(earlier, later):
    peak = jnp.maximum(earlier[0], later[0])
    total = earlier[1] * jnp.exp(earlier[0] - peak) + later[1] * jnp.exp(later[0] - peak)
    return (peak, total, earlier[2] + later[2])


def on_device(
    latent_vectors,
    unembedding_matrix,
    drawn_symbols,
    piece_extents,
    piece_episode_lookup,
    episode_heats,
):
    tok_rows = latent_vectors.shape[0]
    ends = jnp.cumsum(piece_extents[0])
    starts = ends - piece_extents[0]
    position = jnp.arange(tok_rows, dtype=jnp.int32)
    piece_episode = (
        (position[None, :] >= starts[:, None]) & (position[None, :] < ends[:, None])
    ).astype(jnp.float32)
    chosen_symbol = (
        piece_episode_lookup[0][:, None]
        == jnp.arange(episode_heats.shape[0], dtype=jnp.int32)[None, :]
    ).astype(jnp.float32)
    piece_reciprocal_heat = jnp.dot(
        chosen_symbol, 1.0 / episode_heats, precision=lax.Precision.HIGHEST
    )
    symbol_reciprocal_heat = jnp.dot(
        piece_reciprocal_heat, piece_episode, precision=lax.Precision.HIGHEST
    )
    gathered, scale_all, target_all = (
        lax.all_gather(latent_vectors, TOK, axis=0, tiled=True),
        lax.all_gather(symbol_reciprocal_heat, TOK, axis=0, tiled=True),
        lax.all_gather(drawn_symbols, TOK, axis=0, tiled=True),
    )
    width = unembedding_matrix.shape[1]
    column_start = (lax.axis_index(TOK) * lax.axis_size(VOCAB) + lax.axis_index(VOCAB)) * width
    logits = (
        jnp.dot(
            gathered,
            unembedding_matrix,
            preferred_element_type=jnp.float32,
            precision=lax.Precision.HIGHEST,
        )
        * scale_all[:, None]
    )
    ids = column_start + jnp.arange(width, dtype=jnp.int32)
    picked = jnp.sum(jnp.where(target_all[:, None] == ids[None, :], logits, 0.0), axis=1)
    local_top = jnp.max(logits, axis=1)
    local_total = jnp.sum(jnp.exp(logits - local_top[:, None]), axis=1)
    top, total, target_logit = merged_by_axis(
        (local_top, local_total, picked), TOK_VOCAB, combine_pairs
    )
    logprob = target_logit - top - jnp.log(total)
    own = lax.dynamic_slice_in_dim(logprob, lax.axis_index(TOK) * tok_rows, tok_rows, 0)
    sums = jnp.dot(piece_episode, own, precision=lax.Precision.HIGHEST)
    return sums / piece_extents[0].astype(jnp.float32)


def solution(mesh):
    finer = Mesh(mesh.devices.reshape(8, 2, 4, 4), ("tok_0", "tok_1", "vocab_0", "vocab_1"))
    return jax.shard_map(
        on_device,
        mesh=finer,
        in_specs=(P(TOK, None), P(None, TOK_VOCAB), P(TOK), P(TOK, None), P(TOK, None), P()),
        out_specs=P(TOK),
        check_vma=False,
    )
```

profile of v0, /device:TPU:1, one launch (start us, length us, event | category | flops | bytes accessed | tf_op | source)
XLA Modules:
  0.0 239.9 jit_solution(13467237366138529779)
XLA Ops:
  6.5 0.0 all-gather.10.cloned.1.call-start
  6.5 0.7 all-gather.10.cloned.1.call-update
  7.3 0.8 reduce-window.7
  8.1 1.3 dynamic-slice
  10.0 0.7 bitcast_subtract_fusion
  10.7 0.7 broadcast_divide_fusion
  11.4 0.8 convolution_bitcast_fusion.2
  12.2 0.2 convolution_bitcast_fusion.1
  12.4 0.2 dynamic-update-slice
  12.6 0.8 dynamic-update-slice.1
  13.5 29.8 %all-reduce = f32[1536]{0:T(1024)S(1)} all-reduce(f32[1536]{0:T(1024)S(1)} %dynamic-update-slice), channel_id=1, replica_groups=mesh['tok_0'=8,'tok_1'=2,'vocab_0'=4,'vocab_1'=4] {'tok_0','tok_1'}, use_global_device_ids=true, to_apply=%add | all-reduce | flops 1536 | bytes 12288
  43.3 13.1 %all-reduce.1 = s32[1536]{0:T(1024)S(1)} all-reduce(s32[1536]{0:T(1024)S(1)} %dynamic-update-slice.1), channel_id=1, replica_groups=mesh['tok_0'=8,'tok_1'=2,'vocab_0'=4,'vocab_1'=4] {'tok_0','tok_1'}, use_global_device_ids=true, to_apply=%add.1 | all-reduce | flops 1536 | bytes 12288
  56.4 77.9 %all-gather.10.cloned.1.call-done = f32[1536,3584]{1,0:T(8,128)} async-done(((f32[96,3584]{1,0:T(8,128)}), f32[1536,3584]{1,0:T(8,128)}) %all-gather.10.cloned.1.call-update) | async-done | bytes 22020112 | tf_op jit(solution)/shard_map/all_gather | solution.py:70
  134.3 51.2 %fusion.65 = (f32[1536]{0:T(1024)S(1)}, f32[1536,594]{0,1:T(8,128)S(1)}) fusion(f32[1536]{0:T(1024)S(1)} %all-reduce, f32[1536,3584]{1,0:T(8,128)} %all-gather.10.cloned.1.call-done, f32[3584,594]{0,1:T(8,128)} %param.7), kind=kOutput, calls=%fused_computation.134 | convolution fusion | flops 39241633792 | bytes 34197504 | tf_op jit(solution)/shard_map/dot_general | solution.py:77
  185.5 0.0 copy-start
  185.6 0.9 exponential_reduce_fusion
  186.5 18.3 %all-gather.4 = f32[8,3,1536]{2,1,0:T(4,128)S(1)} all-gather(f32[1,3,1536]{2,1,0:T(4,128)S(1)} %maximum_bitcast_fusion), channel_id=2, replica_groups=mesh['tok_0'=8,'tok_1'=2,'vocab_0'=4,'vocab_1'=4] {'tok_0'}, dimensions={0}, use_global_device_ids=true | all-gather | bytes 165888 | tf_op jit(solution)/shard_map/all_gather | solution.py:20
  204.9 0.1 fusion.19
  205.1 8.1 %all-gather.5 = f32[2,3,1536]{2,1,0:T(4,128)S(1)} all-gather(f32[1,3,1536]{2,1,0:T(4,128)S(1)} %maximum_bitcast_fusion.1), channel_id=3, replica_groups=mesh['tok_0'=8,'tok_1'=2,'vocab_0'=4,'vocab_1'=4] {'tok_1'}, dimensions={0}, use_global_device_ids=true | all-gather | bytes 55296 | tf_op jit(solution)/shard_map/all_gather | solution.py:20
  213.3 9.4 %all-gather.6 = f32[4,3,1536]{2,1,0:T(4,128)S(1)} all-gather(f32[1,3,1536]{2,1,0:T(4,128)S(1)} %maximum_bitcast_fusion.2), channel_id=4, replica_groups=mesh['tok_0'=8,'tok_1'=2,'vocab_0'=4,'vocab_1'=4] {'vocab_0'}, dimensions={0}, use_global_device_ids=true | all-gather | bytes 92160 | tf_op jit(solution)/shard_map/all_gather | solution.py:20
  222.7 0.1 fusion.5
  222.8 9.3 %all-gather.7 = f32[4,3,1536]{2,1,0:T(4,128)S(1)} all-gather(f32[1,3,1536]{2,1,0:T(4,128)S(1)} %maximum_bitcast_fusion.3), channel_id=5, replica_groups=mesh['tok_0'=8,'tok_1'=2,'vocab_0'=4,'vocab_1'=4] {'vocab_1'}, dimensions={0}, use_global_device_ids=true | all-gather | bytes 92160 | tf_op jit(solution)/shard_map/all_gather | solution.py:20
  232.1 0.2 slice_reduce_fusion.3
  232.3 0.0 copy-done
  232.4 0.7 fusion
  (17 shorter events, 0.3 us)
Async XLA Ops:
  6.5 127.8 %all-gather.10.cloned.1.call-start = ((), (), s32[]{:S(2)}) async-start(), calls=%async_computation | async-start | bytes 23396352 | tf_op jit(solution)/shard_map/all_gather | solution.py:70
  185.5 46.8 %copy-start = (s32[1,4]{1,0:T(1,128)S(1)}, s32[1,4]{1,0:T(1,128)}, u32[]{:S(2)}) copy-start(s32[1,4]{1,0:T(1,128)} %param.9) | copy-start | bytes 52
Sparse Core Ops, SparseCore 0:
  9.2 125.1 all-gather.9
where the time goes:
time: 244 us; the launch traced here: 240 us
  blocking collectives  88.1 us (36%)
  waiting for transfers between devices  78.6 us (32%)
  matrix products  53 us (22%)
  between operations  14.2 us (6%)
  other arithmetic  3.68 us (2%)
    all_gather x1, waiting for transfers between devices, on_device(): lax.all_gather(latent_vectors, TOK, axis=0, tiled=True)  77.9 us
    dot_general x1, matrix products, on_device(): jnp.dot(gathered, unembedding_matrix, preferred_element_type=jnp.float32,...  51.2 us
    all_gather x4, blocking collectives, collected_together(): both, at, found = (lax.all_gather(jnp.concatenate(lines), axis), 0, {})  45.2 us
    unnamed x2, blocking collectives  42.9 us
  transfers between devices with their start and end apart: 1, of which 1 were waited for; matrix products, arithmetic and copies ran while one was open for 2% of the time, Pallas kernels for 0%

commit v1 on v0

v1 whole, which is shorter than its diff:
```python
import functools

import jax
import jax.numpy as jnp
from jax import lax
from jax.experimental import pallas as pl
from jax.experimental.pallas import tpu as pltpu
from jax.sharding import PartitionSpec as P

MESH = pl.DeviceIdType.MESH

NZ = 8
RING = 4
CH = 8
PIECE = 32
UNIT = 128
UNITS = 12
SLOTS = 14
STEPS = 19
NEG = -3.0e38


def kernel(
    x_hbm, w_hbm, sym_ref, ext_ref, look_ref, heat_ref,
    out_ref,
    X, Wf, Wh, Wl, X2, L, META, MT, MS, RB1, A2, RB2,
    own_sem, w_sem, send_sem, recv_sem, msend, mrecv, s1send, r1, s2send, r2,
):
    div, rem = lax.div, lax.rem
    t = lax.axis_index("tok")
    v = lax.axis_index("vocab")
    z, c = div(t, 2), rem(t, 2)
    y, x = div(v, 4), rem(v, 4)
    a = (1 - c) * x + c * y
    width = w_hbm.shape[1]
    sib = (2 * z + (1 - c), v)

    def along_z(step):
        return (2 * rem(z + step + NZ, NZ) + c, v)

    def along_ring(step):
        to = rem(a + step + RING, RING)
        return (t, (1 - c) * (4 * y + to) + c * (4 * to + x))

    def piece(d, sidx, core, j):
        far = div(d, 4)
        return (1 - far) * (6 + 12 * (d - 1) + 4 * j + 2 * sidx + core) + far * (42 + 2 * j + core)

    def mtile(d, sidx, core):
        far = div(d, 4)
        return (1 - far) * (2 + 4 * (d - 1) + 2 * sidx + core) + far * (14 + core)

    def rows(p, q):
        return X.at[pl.ds(pl.multiple_of(p * PIECE + q * CH, CH), CH), :]

    def send(p_from, p_to, q, device):
        pltpu.make_async_remote_copy(
            src_ref=rows(p_from, q), dst_ref=rows(p_to, q),
            send_sem=send_sem, recv_sem=recv_sem.at[p_to * RING + q],
            device_id=device, device_id_type=MESH,
        ).start()

    def arrived(p, q):
        pltpu.make_async_copy(rows(p, q), rows(p, q), recv_sem.at[p * RING + q]).wait()

    def msg(src, dst, ssem, rsem, device):
        pltpu.make_async_remote_copy(
            src_ref=src, dst_ref=dst, send_sem=ssem, recv_sem=rsem,
            device_id=device, device_id_type=MESH,
        ).start()

    def send_meta(i_from, i_to, device):
        msg(META.at[i_from], META.at[i_to], msend, mrecv.at[i_to], device)

    def meta_arrived(i):
        pltpu.make_async_copy(META.at[i], META.at[i], mrecv.at[i]).wait()

    own = [
        pltpu.make_async_copy(
            x_hbm.at[pl.ds(PIECE * j, PIECE), :],
            X.at[pl.ds(pl.multiple_of((2 * j + c) * PIECE, CH), PIECE), :],
            own_sem.at[j],
        )
        for j in range(3)
    ]
    for copy in own:
        copy.start()
    w_copy = pltpu.make_async_copy(w_hbm, Wf, w_sem)
    w_copy.start()

    barrier = pltpu.get_barrier_semaphore()
    for i in range(1, 16):
        pl.semaphore_signal(barrier, inc=1, device_id=(rem(t + i, 16), v), device_id_type=MESH)
        pl.semaphore_signal(barrier, inc=1, device_id=(t, rem(v + i, 16)), device_id_type=MESH)

    lane = lax.broadcasted_iota(jnp.int32, (1, 128), 1)
    scale_row = jnp.zeros((1, 128), jnp.float32)
    start = 0
    for s in range(4):
        end = start + ext_ref[0, s]
        inv = 1.0 / jnp.full((1, 128), heat_ref[look_ref[0, s]], jnp.float32)
        scale_row = jnp.where((lane >= start) & (lane < end), inv, scale_row)
        start = end
    META[c] = jnp.zeros((8, 128), jnp.float32)
    META[c, 0:1, :] = scale_row
    META[c, 1:2, 0:96] = sym_ref[...].astype(jnp.float32)
    MS[...] = jnp.zeros(MS.shape, jnp.float32)
    MT[...] = jnp.zeros(MT.shape, jnp.float32)

    for copy in own:
        copy.wait()
    pl.semaphore_wait(barrier, 30)

    for k in range(4):
        j = min(k, 2)
        q = rem(a + 2 * (k // 3), RING)
        for sidx, s in enumerate((1, -1)):
            send(2 * j + c, piece(1, sidx, c, j), q, along_z(s))
        if k == 0:
            for sidx, s in enumerate((1, -1)):
                send_meta(c, mtile(1, sidx, c), along_z(s))
            send_meta(c, c, sib)
    for j in range(3):
        for q in range(RING):
            send(2 * j + c, 2 * j + c, q, sib)

    w_copy.wait()
    kblk = 128

    def split_w(i, carry):
        ks = pl.ds(pl.multiple_of(i * kblk, kblk), kblk)
        zero = jnp.zeros((kblk, 128), jnp.bfloat16)
        Wh[ks, 512:640] = zero
        Wl[ks, 512:640] = zero
        for lo, hi in ((0, 256), (256, 512), (512, width)):
            w = Wf[ks, lo:hi]
            high = w.astype(jnp.bfloat16)
            Wh[ks, lo:hi] = high
            Wl[ks, lo:hi] = (w - high.astype(jnp.float32)).astype(jnp.bfloat16)
        return carry

    lax.fori_loop(0, w_hbm.shape[0] // kblk, split_w, 0)
    meta_arrived(1 - c)

    column_start = ((t * 16 + v) * width).astype(jnp.float32)
    depth = X.shape[1]

    def unit(u):
        for i in (0, 2):
            for q in range(RING):
                arrived(4 * u + i + (1 - c), q)
        lanes = lax.broadcasted_iota(jnp.int32, (8, 128), 1)
        tile = jnp.zeros((8, 128), jnp.float32)
        for i in range(4):
            p = 4 * u + i
            near = 1 - jnp.minimum(div(p, 6), 1)
            far = div(p, 42)
            mid = 1 - near - far
            pm = p - 6
            idx = near * (i % 2) + far * (14 + i % 2) + mid * (2 + div(pm, 12) * 4 + rem(pm, 4))
            j = near * div(p, 2) + far * div(p - 42, 2) + mid * div(rem(pm, 12), 4)
            turned = pltpu.roll(META[idx], rem(PIECE * (i - j) + 128, 128), 1)
            tile = jnp.where(div(lanes, PIECE) == i, turned, tile)
        MT[0:8, :] = tile
        columns = MT[...].T
        scale = columns[:, 0:1]
        target = columns[:, 1:2] - column_start

        us = pl.multiple_of(u * UNIT, UNIT)
        for k0 in range(0, depth, 512):
            xs = X[pl.ds(us, UNIT), k0 : k0 + 512]
            high = xs.astype(jnp.bfloat16)
            X2[0:UNIT, k0 : k0 + 512] = high
            X2[UNIT : 2 * UNIT, k0 : k0 + 512] = (xs - high.astype(jnp.float32)).astype(jnp.bfloat16)
        for lo, hi in ((0, 256), (256, 512), (512, 640)):
            both = jnp.dot(X2[...], Wh[:, lo:hi], preferred_element_type=jnp.float32)
            low = jnp.dot(X2[0:UNIT, :], Wl[:, lo:hi], preferred_element_type=jnp.float32)
            L[:, lo:hi] = (both[0:UNIT] + (both[UNIT : 2 * UNIT] + low)) * scale
        col = lax.broadcasted_iota(jnp.int32, (UNIT, 640), 1)
        logits = jnp.where(col < width, L[...], NEG)
        top = jnp.max(logits, axis=1, keepdims=True)
        total = jnp.sum(jnp.exp(logits - top), axis=1, keepdims=True)
        picked = jnp.sum(jnp.where(col.astype(jnp.float32) == target, L[...], 0.0), axis=1, keepdims=True)
        lse = top + jnp.log(total)
        col = lax.broadcasted_iota(jnp.int32, (UNIT, 128), 1)
        flat = jnp.where(col == 0, lse, jnp.where(col == 1, picked, 0.0)).T
        lse_row, picked_row = flat[0:1, :], flat[1:2, :]

        def note(k, row):
            MS[k, pl.ds(row, 1), :] = lse_row
            MS[k, pl.ds(row + 3, 1), :] = picked_row

        @pl.when((u >= 1) & (u <= 9))
        def _():
            note(2 * div(u - 1, 3), rem(u - 1, 3))

        @pl.when((u >= 2) & (u <= 10))
        def _():
            note(2 * div(u - 2, 3) + 1, rem(u - 2, 3))

        @pl.when(u >= 10)
        def _():
            note(6, u - 10)

        @pl.when(u <= 1)
        def _():
            note(7, u)

        def report(d, sidx, s):
            for core in range(2):
                msg(
                    MS.at[2 * (d - 1) + sidx], RB1.at[4 * (d - 1) + 2 * sidx + c],
                    s1send, r1.at[4 * (d - 1) + 2 * sidx + c],
                    (2 * rem(z - s * d + NZ, NZ) + core, v),
                )

        @pl.when(u == 1)
        def _():
            msg(MS.at[7], RB1.at[14], s1send, r1.at[14], sib)

        @pl.when((u >= 3) & (u <= 9) & (rem(u, 3) == 0))
        def _():
            report(div(u, 3), 0, 1)

        @pl.when((u >= 4) & (u <= 10) & (rem(u, 3) == 1))
        def _():
            report(div(u, 3), 1, -1)

    def slot(m, sidx):
        late = div(m, 12)
        k = (1 - late) * rem(m, 4) + late * (2 * (m - 12) + sidx)
        return 1 + div(m, 4), k

    def step(n, carry):
        @pl.when((n >= 2) & (n < SLOTS + 2))
        def _():
            m = n - 2
            for sidx in range(2):
                d, k = slot(m, sidx)

                @pl.when(k < 3)
                def _():
                    p = piece(d, sidx, c, k)
                    for gi, g in enumerate((1, -1)):
                        q = rem(a - g + RING, RING)
                        arrived(p, q)

                        @pl.when(k == gi)
                        def _():
                            send(p, p, q, along_ring(g))

                        send(p, p, q, sib)

        @pl.when(n < SLOTS)
        def _():
            for sidx, s in enumerate((1, -1)):
                d, k = slot(n, sidx)
                extra = div(k, 3)
                j = k - extra
                q = rem(a + 2 * extra, RING)
                p = piece(d, sidx, c, j)
                arrived(p, q)

                @pl.when((d < 3) | ((d == 3) & (rem(k, 2) == sidx)))
                def _():
                    send(p, piece(d + 1, sidx, c, j), q, along_z(s))

                @pl.when(k < 3)
                def _():
                    send(p, p, q, along_ring(1))
                    send(p, p, q, along_ring(-1))

                send(p, p, q, sib)

                @pl.when((rem(n, 4) == 0) & (d < 5 - sidx))
                def _():
                    i = mtile(d, sidx, c)
                    meta_arrived(i)

                    @pl.when(d < 4 - sidx)
                    def _():
                        send_meta(i, mtile(d + 1, sidx, c), along_z(s))

                    send_meta(i, i, sib)

        @pl.when((n >= 1) & (n < SLOTS) & (rem(n + 3, 4) == 0))
        def _():
            d = 1 + div(n - 1, 4)
            meta_arrived(mtile(d, 0, 1 - c))

            @pl.when(d < 4)
            def _():
                meta_arrived(mtile(d, 1, 1 - c))

        @pl.when((n >= 4) & (n < SLOTS + 4))
        def _():
            m = n - 4
            for sidx in range(2):
                d, k = slot(m, sidx)

                @pl.when(k < 2)
                def _():
                    p = piece(d, sidx, c, k)
                    q = rem(a + 2, RING)
                    arrived(p, q)
                    send(p, p, q, sib)

        r = n - 5

        @pl.when((n == 4) | ((n >= 5) & (rem(r + 4, 4) < 3)))
        def _():
            first = div(n, 5)
            late = jnp.minimum(first, 1)
            unit(late * (1 + div(r, 4) * 3 + rem(r, 4)))

        return carry

    lax.fori_loop(0, STEPS, step, 0)

    for core in range(2):
        msg(MS.at[6], RB1.at[12 + c], s1send, r1.at[12 + c], (2 * rem(z + 4, NZ) + core, v))
    pltpu.make_async_copy(X.at[pl.ds(0, 180 * CH), :], X.at[pl.ds(0, 180 * CH), :], send_sem).wait()
    pltpu.make_async_copy(META.at[pl.ds(0, 15)], META.at[pl.ds(0, 15)], msend).wait()

    def lse_of(values):
        peak = functools.reduce(jnp.maximum, values)
        return peak + jnp.log(sum(jnp.exp(value - peak) for value in values))

    subl = lax.broadcasted_iota(jnp.int32, (8, 128), 0)

    def merged(tiles):
        return jnp.where(subl < 3, lse_of(tiles), sum(tiles))

    def r1_arrived(i):
        pltpu.make_async_copy(RB1.at[i], RB1.at[i], r1.at[i]).wait()

    for i in range(12):
        r1_arrived(i)
    r1_arrived(14)
    up = pltpu.roll(merged([RB1[4 * k + i] for k in range(3) for i in (0, 1)]), 64, 1)
    down = merged([RB1[4 * k + i] for k in range(3) for i in (2, 3)])
    here = merged([RB1[14], MS[7]])
    hr = pltpu.roll(here, 64, 1)
    near = jnp.where(rem(subl, 3) == 0, here, jnp.where(rem(subl, 3) == 1, pltpu.roll(hr, 1, 0), pltpu.roll(here, 1, 0)))
    first = merged([up, down, near])
    for i in range(12, 14):
        r1_arrived(i)
    there = merged([RB1[12], RB1[13]])
    tr = pltpu.roll(there, 64, 1)
    away = jnp.where(rem(subl, 3) == 0, tr, jnp.where(rem(subl, 3) == 1, there, pltpu.roll(tr, 1, 0)))
    A2[...] = merged([first, away])

    for i in range(1, 16):
        msg(A2, RB2.at[i - 1], s2send, r2.at[i - 1], (t, rem(v + i, 16)))
    pltpu.make_async_copy(RB1.at[pl.ds(0, 15)], RB1.at[pl.ds(0, 15)], s1send).wait()
    for i in range(15):
        pltpu.make_async_copy(RB2.at[i], RB2.at[i], r2.at[i]).wait()
    final = merged([A2[...]] + [RB2[i] for i in range(15)])
    logprob = pltpu.roll(final, 5, 0) - final
    lanes = lax.broadcasted_iota(jnp.int32, (8, 128), 1)
    inside = (div(lanes, PIECE) == c) & (subl < 3)
    position = subl * PIECE + rem(lanes, PIECE)
    result = jnp.zeros((8, 128), jnp.float32)
    start = 0
    for s in range(4):
        size = ext_ref[0, s]
        mask = inside & (position >= start) & (position < start + size)
        value = jnp.sum(jnp.where(mask, logprob, 0.0)) / size.astype(jnp.float32)
        result = jnp.where(lanes == s, value, result)
        start = start + size
    out_ref[...] = result
    pltpu.make_async_copy(RB2, RB2, s2send).wait()


def on_device(latent_vectors, unembedding_matrix, drawn_symbols, piece_extents, piece_episode_lookup, episode_heats):
    rows, depth = latent_vectors.shape
    width = unembedding_matrix.shape[1]
    f32, bf16 = jnp.float32, jnp.bfloat16
    dma, vmem, smem = pltpu.SemaphoreType.DMA, pltpu.VMEM, pltpu.SMEM
    out = pl.pallas_call(
        kernel,
        out_shape=jax.ShapeDtypeStruct((8, 128), f32),
        in_specs=[
            pl.BlockSpec(memory_space=pl.ANY),
            pl.BlockSpec(memory_space=pl.ANY),
            pl.BlockSpec(memory_space=vmem),
            pl.BlockSpec(memory_space=smem),
            pl.BlockSpec(memory_space=smem),
            pl.BlockSpec(memory_space=smem),
        ],
        out_specs=pl.BlockSpec(memory_space=vmem),
        scratch_shapes=[
            vmem((16 * rows, depth), f32),
            vmem((depth, width), f32),
            vmem((depth, 640), bf16),
            vmem((depth, 640), bf16),
            vmem((2 * UNIT, depth), bf16),
            vmem((UNIT, 640), f32),
            vmem((16, 8, 128), f32),
            vmem((128, 128), f32),
            vmem((8, 8, 128), f32),
            vmem((15, 8, 128), f32),
            vmem((8, 128), f32),
            vmem((15, 8, 128), f32),
            dma((3,)), dma, dma, dma((192,)), dma, dma((16,)), dma, dma((15,)), dma, dma((15,)),
        ],
        compiler_params=pltpu.CompilerParams(
            collective_id=0, has_side_effects=True, vmem_limit_bytes=60 * 1024 * 1024
        ),
    )(
        latent_vectors, unembedding_matrix, drawn_symbols.reshape(1, rows),
        piece_extents, piece_episode_lookup, episode_heats,
    )
    return out[0, :4]


def solution(mesh):
    return jax.shard_map(
        on_device,
        mesh=mesh,
        in_specs=(P("tok", None), P(None, ("tok", "vocab")), P("tok"), P("tok", None), P("tok", None), P()),
        out_specs=P("tok"),
        check_vma=False,
    )
```

time: 244 us -> 96.2 us (0.39); the launches traced: 240 us -> 95.9 us
  blocking collectives: 88.1 us -> 0 us
  Pallas kernels: 0 us -> 84 us
  waiting for transfers between devices: 78.6 us -> 0 us
  matrix products: 53 us -> 0 us
  between operations: 14.2 us -> 0.01 us
  local copies, waits for them, and re-layouts: 2.34 us -> 11.9 us
  other arithmetic: 3.68 us -> 0 us
    pallas_call x0 -> x1, Pallas kernels: none -> 84 us  [on_device(): pl.pallas_call(kernel, out_shape=jax.ShapeDtypeStruct((8, 128), f32), in_...]
    all_gather x1 -> x0, waiting for transfers between devices: 77.9 us -> none  [on_device(): lax.all_gather(latent_vectors, TOK, axis=0, tiled=True)]
    dot_general x4 -> x0, matrix products: 53 us -> none  [the longest x1 51.2 us: on_device(): jnp.dot(gathered, unembedding_matrix, preferred_element_type=jnp.float32,...]
    all_gather x4 -> x0, blocking collectives: 45.2 us -> none  [collected_together(): both, at, found = (lax.all_gather(jnp.concatenate(lines), axis), 0, {})]
    unnamed x2 -> x0, blocking collectives: 42.9 us -> none
    unnamed x7 -> x1, local copies, waits for them, and re-layouts: 2.33 us -> 10.7 us
  transfers between devices with their start and end apart: 1 -> 0, of which waited for: 1 -> 0; matrix products, arithmetic and copies ran while one was open for 2% -> 0% of each run, Pallas kernels for 0% -> 0%
where the time goes in v1:
time: 96.2 us; the launch traced here: 95.9 us
  Pallas kernels  84 us (87%)
  local copies, waits for them, and re-layouts  11.9 us (12%)
    pallas_call x1, Pallas kernels, on_device(): pl.pallas_call(kernel, out_shape=jax.ShapeDtypeStruct((8, 128), f32), in_...  84 us
    unnamed x1, local copies, waits for them, and re-layouts  10.7 us

profile of v1, /device:TPU:1, one launch (start us, length us, event | category | flops | bytes accessed | tf_op | source)
XLA Modules:
  0.0 95.9 jit_solution(3252378283625984144)
XLA Ops:
  0.0 10.7 %copy.7.w_hbm = f32[3584,594]{1,0:T(8,128)} copy(f32[3584,594]{0,1:T(8,128)} %param.7) | data formatting | bytes 17031168 | tf_op args[1]
  10.7 84.0 %shard_map.64 = f32[8,128]{1,0:T(8,128)} custom-call(f32[96,3584]{1,0:T(8,128)} %x_hbm.1, f32[3584,594]{1,0:T(8,128)} %copy.7.w_hbm, s32[1,96]{1,0:T(1,128)} %bitcast.3, s32[1,4]{1,0:T(1,128)} %ext_ref.1, s32[1,4]{1,0:T(1,128)} %look_ref.1, f32[1024]{0:T(1024)} %heat_ref.1), custom_call_target="tpu_custom_call" | custom-call | tf_op jit(solution)/shard_map/pallas_call | solution.py:380
  94.7 1.2 %slice_bitcast_fusion = f32[4]{0:T(128)} fusion(f32[8,128]{1,0:T(8,128)} %shard_map.64), kind=kLoop, calls=%fused_computation | loop fusion | bytes 32 | tf_op jit(solution)/shard_map/squeeze | solution.py:414

commit v2 on v1

v2 whole, which is shorter than its diff:
```python
import functools

import jax
import jax.numpy as jnp
from jax import lax
from jax.experimental import pallas as pl
from jax.experimental.pallas import tpu as pltpu
from jax.sharding import PartitionSpec as P

MESH = pl.DeviceIdType.MESH

NZ = 8
RING = 4
CH = 8
PIECE = 32
UNIT = 128
UNITS = 12
SLOTS = 14
STEPS = 19
NEG = -3.0e38
F8 = jnp.float8_e4m3fn
X_UP, W_UP = 2.0**8, 2.0**12
W_EARLY = 20


def kernel(
    x_hbm, wt_hbm, sym_hbm, ext_hbm, look_hbm, heat_hbm,
    out_ref,
    sym_ref, ext_ref, look_ref, heat_ref, X, Wf, Wh, W8, X2, X8, L, META, MT, MS, RB1, A2, RB2,
    own_sem, small_sem, w_sem, send_sem, recv_sem, msend, mrecv, s1send, r1, s2send, r2,
):
    div, rem = lax.div, lax.rem
    t = lax.axis_index("tok")
    v = lax.axis_index("vocab")
    z, c = div(t, 2), rem(t, 2)
    y, x = div(v, 4), rem(v, 4)
    a = (1 - c) * x + c * y
    width, depth = wt_hbm.shape
    sib = (2 * z + (1 - c), v)

    z_dev = {s: (2 * rem(z + s + NZ, NZ) + c, v) for s in (1, -1)}
    turn = [rem(a + s, RING) for s in range(RING)]
    ring_dev = {s: (t, (1 - c) * (4 * y + turn[s % RING]) + c * (4 * turn[s % RING] + x)) for s in (1, -1, 2)}

    def own_piece(core, j):
        return 2 * j + core if j < 2 else 40 + core

    def piece(d, sidx, core, j):
        far = div(d, 4)
        return (1 - far) * (4 + 12 * (d - 1) + 4 * j + 2 * sidx + core) + far * (44 + 2 * j - 6 * div(j, 2) + core)

    def mtile(d, sidx, core):
        far = div(d, 4)
        return (1 - far) * (2 + 4 * (d - 1) + 2 * sidx + core) + far * (14 + core)

    def rows(p, q):
        return X.at[pl.ds(pl.multiple_of(p * PIECE + q * CH, CH), CH), :]

    def send(p_from, p_to, q, device):
        pltpu.make_async_remote_copy(
            src_ref=rows(p_from, q), dst_ref=rows(p_to, q),
            send_sem=send_sem, recv_sem=recv_sem.at[p_to * RING + q],
            device_id=device, device_id_type=MESH,
        ).start()

    def arrived(p, q):
        pltpu.make_async_copy(rows(p, q), rows(p, q), recv_sem.at[p * RING + q]).wait()

    def msg(src, dst, ssem, rsem, device):
        pltpu.make_async_remote_copy(
            src_ref=src, dst_ref=dst, send_sem=ssem, recv_sem=rsem,
            device_id=device, device_id_type=MESH,
        ).start()

    def send_meta(i_from, i_to, device):
        msg(META.at[i_from], META.at[i_to], msend, mrecv.at[i_to], device)

    def meta_arrived(i):
        pltpu.make_async_copy(META.at[i], META.at[i], mrecv.at[i]).wait()

    barrier = pltpu.get_barrier_semaphore()
    for i in range(1, 16):
        pl.semaphore_signal(barrier, inc=1, device_id=(rem(t + i, 16), v), device_id_type=MESH)
        pl.semaphore_signal(barrier, inc=1, device_id=(t, rem(v + i, 16)), device_id_type=MESH)
    own = [
        pltpu.make_async_copy(
            x_hbm.at[pl.ds(PIECE * j, PIECE), :],
            X.at[pl.ds(pl.multiple_of(own_piece(c, j) * PIECE, CH), PIECE), :],
            own_sem.at[j],
        )
        for j in range(3)
    ]
    small = [
        pltpu.make_async_copy(src, dst, small_sem.at[k])
        for k, (src, dst) in enumerate(
            ((sym_hbm, sym_ref), (ext_hbm, ext_ref), (look_hbm, look_ref), (heat_hbm, heat_ref))
        )
    ]
    w_copy = pltpu.make_async_copy(wt_hbm, Wf, w_sem)
    for copy in own + small + [w_copy]:
        copy.start()
    for copy in small:
        copy.wait()
    lane = lax.broadcasted_iota(jnp.int32, (1, 128), 1)
    scale_row = jnp.zeros((1, 128), jnp.float32)
    start = 0
    for s in range(4):
        end = start + ext_ref[0, s]
        inv = 1.0 / jnp.full((1, 128), heat_ref[look_ref[0, s]], jnp.float32)
        scale_row = jnp.where((lane >= start) & (lane < end), inv, scale_row)
        start = end
    META[c] = jnp.zeros((8, 128), jnp.float32)
    META[c, 0:1, :] = scale_row
    META[c, 1:2, 0:96] = sym_ref[...].astype(jnp.float32)
    MS[...] = jnp.zeros(MS.shape, jnp.float32)
    MT[...] = jnp.zeros(MT.shape, jnp.float32)
    for copy in own:
        copy.wait()
    pl.semaphore_wait(barrier, 30)

    for sidx, s in enumerate((1, -1)):
        send_meta(c, mtile(1, sidx, c), z_dev[s])
    send_meta(c, c, sib)
    for k in range(4):
        j = min(k, 2)
        q = turn[2 * (k // 3)]
        for sidx, s in enumerate((1, -1)):
            send(own_piece(c, j), piece(1, sidx, c, j), q, z_dev[s])
    for j in range(3):
        for q in range(RING):
            send(own_piece(c, j), own_piece(c, j), q, sib)

    w_copy.wait()

    twice = 640 - width

    def split_w(i, carry):
        ks = pl.ds(pl.multiple_of(i * 128, 128), 128)
        kt = pl.ds(pl.multiple_of(depth + i * 128, 128), 128)
        for b in range(5):
            w = Wf[min(128 * b, width - 128) : min(128 * b + 128, width), ks].T
            at = slice(128 * b, 128 * b + 128)
            high = w.astype(jnp.bfloat16)
            Wh[ks, at] = high
            W8[ks, at] = (w * W_UP).astype(F8)
            W8[kt, at] = ((w - high.astype(jnp.float32)) * (W_UP * X_UP)).astype(F8)
        return carry

    lax.fori_loop(0, W_EARLY, split_w, 0)
    meta_arrived(1 - c)

    column_start = ((t * 16 + v) * width).astype(jnp.float32)

    def unit(u):
        for i in (0, 2):
            for q in range(RING):
                arrived(4 * u + i + (1 - c), q)
        lanes = lax.broadcasted_iota(jnp.int32, (8, 128), 1)
        tile = jnp.zeros((8, 128), jnp.float32)
        first, last = 1 - jnp.minimum(u, 1), div(u, 11)
        ten = div(u, 10) - last
        mid = 1 - first - last - ten
        for i in range(4):
            idx = first * (i % 2) + mid * (2 + 4 * div(u - 1, 3) + i) + ten * (i if i < 2 else 12 + i) + last * (14 + i % 2)
            j = (first + last) * (i // 2) + mid * rem(u + 2, 3) + ten * 2
            turned = pltpu.roll(META[idx], rem(PIECE * (i - j) + 128, 128), 1)
            tile = jnp.where(div(lanes, PIECE) == i, turned, tile)
        MT[0:8, :] = tile
        columns = MT[...].T
        scale = columns[:, 0:1]
        target = columns[:, 1:2] - column_start

        us = pl.multiple_of(u * UNIT, UNIT)
        for k0 in range(0, depth, 512):
            xs = X[pl.ds(us, UNIT), k0 : k0 + 512]
            high = xs.astype(jnp.bfloat16)
            X2[:, k0 : k0 + 512] = high
            X8[:, k0 : k0 + 512] = ((xs - high.astype(jnp.float32)) * X_UP).astype(F8)
            X8[:, depth + k0 : depth + k0 + 512] = xs.astype(F8)
        for lo, hi in ((0, 256), (256, 512), (512, 640)):
            main = jnp.dot(X2[...], Wh[:, lo:hi], preferred_element_type=jnp.float32)
            rest = jnp.dot(X8[...], W8[:, lo:hi], preferred_element_type=jnp.float32)
            L[:, lo:hi] = (main + rest * (1.0 / (W_UP * X_UP))) * scale
        col = lax.broadcasted_iota(jnp.int32, (1, 640), 1)
        col = jnp.where(col < 512, col, jnp.where(col < 512 + twice, -(1 << 24), col - twice))
        logits = jnp.where(col >= 0, L[...], NEG)
        top = jnp.max(logits, axis=1, keepdims=True)
        total = jnp.sum(jnp.exp(logits - top), axis=1, keepdims=True)
        picked = jnp.sum(jnp.where(col.astype(jnp.float32) == target, logits, 0.0), axis=1, keepdims=True)
        lse = top + jnp.log(total)
        col = lax.broadcasted_iota(jnp.int32, (UNIT, 128), 1)
        flat = jnp.where(col == 0, lse, jnp.where(col == 1, picked, 0.0)).T
        lse_row, picked_row = flat[0:1, :], flat[1:2, :]

        def note(k, row):
            MS[k, pl.ds(row, 1), :] = lse_row
            MS[k, pl.ds(row + 3, 1), :] = picked_row

        @pl.when((u >= 1) & (u <= 9))
        def _():
            note(div(u - 1, 3), rem(u + 2, 3))

        @pl.when(u >= 10)
        def _():
            note(3, 11 - u)

        @pl.when((u == 0) | (u == 10))
        def _():
            note(4, div(u, 10))

        @pl.when(u == 10)
        def _():
            msg(MS.at[4], RB1.at[14], s1send, r1.at[14], sib)

        @pl.when((u >= 1) & (u <= 9) & (rem(u, 3) == 2))
        def _():
            d = 1 + div(u - 1, 3)
            for sidx, s in enumerate((1, -1)):
                for core in range(2):
                    i = 4 * (d - 1) + 2 * sidx + c
                    msg(MS.at[d - 1], RB1.at[i], s1send, r1.at[i], (2 * rem(z - s * d + NZ, NZ) + core, v))

    def slot(m, sidx):
        late = div(m, 12)
        k = (1 - late) * rem(m, 4) + late * (2 * (m - 12) + sidx)
        return 1 + div(m, 4), k

    def step(n, carry):
        @pl.when(n < SLOTS)
        def _():
            for sidx, s in enumerate((1, -1)):
                d, k = slot(n, sidx)
                extra = div(k, 3)
                j = k - extra
                q = (1 - extra) * a + extra * turn[2]
                p = piece(d, sidx, c, j)
                arrived(p, q)

                @pl.when((d < 3) | ((d == 3) & (rem(k, 2) == sidx)))
                def _():
                    send(p, piece(d + 1, sidx, c, j), q, z_dev[s])

                @pl.when(k < 3)
                def _():
                    send(p, p, q, ring_dev[1])
                    send(p, p, q, ring_dev[-1])

                @pl.when((k < 2) & (d == 4))
                def _():
                    send(p, p, q, ring_dev[2])

                send(p, p, q, sib)

                @pl.when((rem(n, 4) == 0) & (d < 5 - sidx))
                def _():
                    i = mtile(d, sidx, c)
                    meta_arrived(i)

                    @pl.when(d < 4 - sidx)
                    def _():
                        send_meta(i, mtile(d + 1, sidx, c), z_dev[s])

                    send_meta(i, i, sib)

        @pl.when((n >= 2) & (n < SLOTS + 3) & (n != 14))
        def _():
            m = n - 2 - div(n, 15)
            for sidx in range(2):
                d, k = slot(m, sidx)

                @pl.when(k < 3)
                def _():
                    p = piece(d, sidx, c, k)
                    for gi, g in enumerate((1, -1)):
                        q = turn[-g % RING]
                        arrived(p, q)

                        @pl.when((k == gi) & (d < 4))
                        def _():
                            send(p, p, q, ring_dev[g])

                        send(p, p, q, sib)

        @pl.when((n >= 1) & (n < SLOTS) & (rem(n + 3, 4) == 0))
        def _():
            d = 1 + div(n - 1, 4)
            meta_arrived(mtile(d, 0, 1 - c))

            @pl.when(d < 4)
            def _():
                meta_arrived(mtile(d, 1, 1 - c))

        @pl.when((n >= 5) & (n < SLOTS + 5))
        def _():
            m = n - 5
            for sidx in range(2):
                d, k = slot(m, sidx)

                @pl.when(k < 2)
                def _():
                    p = piece(d, sidx, c, k)
                    q = turn[2]
                    arrived(p, q)
                    send(p, p, q, sib)

        @pl.when(n == 0)
        def _():
            lax.fori_loop(W_EARLY, depth // 128, split_w, 0)

        r = n - 5

        @pl.when((n == 0) | ((n >= 5) & (rem(r + 4, 4) < 3)))
        def _():
            some, late = jnp.minimum(n, 1), div(n, 17)
            unit(some * ((1 - late) * (1 + 3 * div(r, 4) + rem(rem(r + 4, 4) + 2, 3)) + late * (n - 7)))

        return carry

    lax.fori_loop(0, STEPS, step, 0)

    for core in range(2):
        msg(MS.at[3], RB1.at[12 + c], s1send, r1.at[12 + c], (2 * rem(z + 4, NZ) + core, v))
    pltpu.make_async_copy(X.at[pl.ds(0, 180 * CH), :], X.at[pl.ds(0, 180 * CH), :], send_sem).wait()
    pltpu.make_async_copy(META.at[pl.ds(0, 15)], META.at[pl.ds(0, 15)], msend).wait()

    def lse_of(values):
        peak = functools.reduce(jnp.maximum, values)
        return peak + jnp.log(sum(jnp.exp(value - peak) for value in values))

    subl = lax.broadcasted_iota(jnp.int32, (8, 128), 0)

    def merged(tiles):
        return jnp.where(subl < 3, lse_of(tiles), sum(tiles))

    def r1_arrived(i):
        pltpu.make_async_copy(RB1.at[i], RB1.at[i], r1.at[i]).wait()

    for i in range(12):
        r1_arrived(i)
    r1_arrived(14)
    up = merged([RB1[4 * k + i] for k in range(3) for i in (0, 1)])
    down = pltpu.roll(merged([RB1[4 * k + i] for k in range(3) for i in (2, 3)]), 64, 1)
    here = merged([RB1[14], MS[4]])
    hr = pltpu.roll(here, 64, 1)
    near = jnp.where(rem(subl, 3) == 0, here, jnp.where(rem(subl, 3) == 1, pltpu.roll(hr, 1, 0), pltpu.roll(here, 1, 0)))
    first = merged([up, down, near])
    for i in range(12, 14):
        r1_arrived(i)
    there = merged([RB1[12], RB1[13]])
    tr = pltpu.roll(there, 64, 1)
    away = jnp.where(rem(subl, 3) == 0, there, pltpu.roll(tr, 1, 0))
    A2[...] = merged([first, away])

    for i in range(1, 16):
        msg(A2, RB2.at[i - 1], s2send, r2.at[i - 1], (t, rem(v + i, 16)))
    pltpu.make_async_copy(RB1.at[pl.ds(0, 15)], RB1.at[pl.ds(0, 15)], s1send).wait()
    for i in range(15):
        pltpu.make_async_copy(RB2.at[i], RB2.at[i], r2.at[i]).wait()
    final = merged([A2[...]] + [RB2[i] for i in range(15)])
    logprob = pltpu.roll(final, 5, 0) - final
    lanes = lax.broadcasted_iota(jnp.int32, (8, 128), 1)
    inside = (div(lanes, PIECE) == c) & (subl < 3)
    position = subl * PIECE + rem(lanes, PIECE)
    result = jnp.zeros((8, 128), jnp.float32)
    start = 0
    for s in range(4):
        size = ext_ref[0, s]
        mask = inside & (position >= start) & (position < start + size)
        value = jnp.sum(jnp.where(mask, logprob, 0.0)) / size.astype(jnp.float32)
        result = jnp.where(lanes == s, value, result)
        start = start + size
    out_ref[...] = result
    pltpu.make_async_copy(RB2, RB2, s2send).wait()


def on_device(latent_vectors, unembedding_matrix, drawn_symbols, piece_extents, piece_episode_lookup, episode_heats):
    rows, depth = latent_vectors.shape
    width = unembedding_matrix.shape[1]
    f32, bf16 = jnp.float32, jnp.bfloat16
    dma, vmem, smem = pltpu.SemaphoreType.DMA, pltpu.VMEM, pltpu.SMEM
    out = pl.pallas_call(
        kernel,
        out_shape=jax.ShapeDtypeStruct((8, 128), f32),
        in_specs=[pl.BlockSpec(memory_space=pl.ANY)] * 6,
        out_specs=pl.BlockSpec(memory_space=vmem),
        scratch_shapes=[
            vmem((1, rows), jnp.int32),
            smem(piece_extents.shape, jnp.int32),
            smem(piece_episode_lookup.shape, jnp.int32),
            smem(episode_heats.shape, f32),
            vmem((16 * rows, depth), f32),
            vmem((width, depth), f32),
            vmem((depth, 640), bf16),
            vmem((2 * depth, 640), F8),
            vmem((UNIT, depth), bf16),
            vmem((UNIT, 2 * depth), F8),
            vmem((UNIT, 640), f32),
            vmem((16, 8, 128), f32),
            vmem((128, 128), f32),
            vmem((8, 8, 128), f32),
            vmem((15, 8, 128), f32),
            vmem((8, 128), f32),
            vmem((15, 8, 128), f32),
            dma((3,)), dma((4,)), dma, dma, dma((192,)), dma, dma((16,)), dma, dma((15,)), dma, dma((15,)),
        ],
        compiler_params=pltpu.CompilerParams(
            collective_id=0, has_side_effects=True, vmem_limit_bytes=60 * 1024 * 1024
        ),
    )(
        latent_vectors, unembedding_matrix.T, drawn_symbols.reshape(1, rows),
        piece_extents, piece_episode_lookup, episode_heats,
    )
    return out[0, :4]


def solution(mesh):
    return jax.shard_map(
        on_device,
        mesh=mesh,
        in_specs=(P("tok", None), P(None, ("tok", "vocab")), P("tok"), P("tok", None), P("tok", None), P()),
        out_specs=P("tok"),
        check_vma=False,
    )
```

time: 96.2 us -> 74.2 us (0.77)
  Pallas kernels: 84 us -> 72.9 us
  local copies, waits for them, and re-layouts: 11.9 us -> 1.19 us
    pallas_call x1, Pallas kernels: 84 us -> 72.9 us  [on_device(): pl.pallas_call(kernel, out_shape=jax.ShapeDtypeStruct((8, 128), f32), in_...]
    unnamed x1 -> x0, local copies, waits for them, and re-layouts: 10.7 us -> none
where the time goes in v2:
time: 74.2 us; the launch traced here: 74.1 us
  Pallas kernels  72.9 us (98%)
  local copies, waits for them, and re-layouts  1.19 us (2%)
    pallas_call x1, Pallas kernels, on_device(): pl.pallas_call(kernel, out_shape=jax.ShapeDtypeStruct((8, 128), f32), in_...  72.9 us

profile of v2, /device:TPU:1, one launch (start us, length us, event | category | flops | bytes accessed | tf_op | source)
XLA Modules:
  0.0 74.1 jit_solution(2689571457515595947)
XLA Ops:
  0.0 72.9 %shard_map.64 = f32[8,128]{1,0:T(8,128)} custom-call(f32[96,3584]{1,0:T(8,128)} %x_hbm.1, f32[594,3584]{1,0:T(8,128)} %bitcast.4, s32[1,96]{1,0:T(1,128)} %bitcast.5, s32[1,4]{1,0:T(1,128)} %ext_hbm.1, s32[1,4]{1,0:T(1,128)} %look_hbm.1, f32[1024]{0:T(1024)} %heat_hbm.1), custom_call_target="tpu_custom_call" | custom-call | tf_op jit(solution)/shard_map/pallas_call | solution.py:381
  72.9 1.2 %slice_bitcast_fusion = f32[4]{0:T(128)} fusion(f32[8,128]{1,0:T(8,128)} %shard_map.64), kind=kLoop, calls=%fused_computation | loop fusion | bytes 32 | tf_op jit(solution)/shard_map/squeeze | solution.py:413

commit v3 on v2

--- a/solution.py
+++ b/solution.py
@@ -16,11 +16,11 @@
 UNIT = 128
 UNITS = 12
 SLOTS = 14
-STEPS = 19
+STEPS = 18
 NEG = -3.0e38
 F8 = jnp.float8_e4m3fn
 X_UP, W_UP = 2.0**8, 2.0**12
-W_EARLY = 20
+W_EARLY, W_STEP = 16, 6
 
 
 def kernel(
@@ -290,9 +290,9 @@
             def _():
                 meta_arrived(mtile(d, 1, 1 - c))
 
-        @pl.when((n >= 5) & (n < SLOTS + 5))
-        def _():
-            m = n - 5
+        @pl.when((n >= 6) & (n < 16))
+        def _():
+            m = n - 6 + div(n, 13) + 2 * div(n, 15)
             for sidx in range(2):
                 d, k = slot(m, sidx)
 
@@ -303,16 +303,19 @@
                     arrived(p, q)
                     send(p, p, q, sib)
 
-        @pl.when(n == 0)
-        def _():
-            lax.fori_loop(W_EARLY, depth // 128, split_w, 0)
+        @pl.when(n < 2)
+        def _():
+            at = W_EARLY + n * W_STEP
+            lax.fori_loop(at, at + W_STEP, split_w, 0)
 
         r = n - 5
-
-        @pl.when((n == 0) | ((n >= 5) & (rem(r + 4, 4) < 3)))
-        def _():
-            some, late = jnp.minimum(n, 1), div(n, 17)
-            unit(some * ((1 - late) * (1 + 3 * div(r, 4) + rem(rem(r + 4, 4) + 2, 3)) + late * (n - 7)))
+        quarter = rem(r + 4, 4)
+
+        @pl.when((n == 2) | ((n >= 5) & (quarter != 1)) | (n >= 14))
+        def _():
+            some, late, end = jnp.minimum(div(n, 3), 1), div(n, 14), div(n, 16)
+            usual = 1 + 3 * div(r, 4) + rem(quarter + 2, 4)
+            unit(some * ((1 - late) * usual + (late - end) * (n - 7) + end * (27 - n)))
 
         return carry
 
@@ -361,15 +364,12 @@
     lanes = lax.broadcasted_iota(jnp.int32, (8, 128), 1)
     inside = (div(lanes, PIECE) == c) & (subl < 3)
     position = subl * PIECE + rem(lanes, PIECE)
-    result = jnp.zeros((8, 128), jnp.float32)
     start = 0
     for s in range(4):
         size = ext_ref[0, s]
         mask = inside & (position >= start) & (position < start + size)
-        value = jnp.sum(jnp.where(mask, logprob, 0.0)) / size.astype(jnp.float32)
-        result = jnp.where(lanes == s, value, result)
+        out_ref[s] = jnp.sum(jnp.where(mask, logprob, 0.0)) / size.astype(jnp.float32)
         start = start + size
-    out_ref[...] = result
     pltpu.make_async_copy(RB2, RB2, s2send).wait()
 
 
@@ -380,9 +380,9 @@
     dma, vmem, smem = pltpu.SemaphoreType.DMA, pltpu.VMEM, pltpu.SMEM
     out = pl.pallas_call(
         kernel,
-        out_shape=jax.ShapeDtypeStruct((8, 128), f32),
+        out_shape=jax.ShapeDtypeStruct((4,), f32),
         in_specs=[pl.BlockSpec(memory_space=pl.ANY)] * 6,
-        out_specs=pl.BlockSpec(memory_space=vmem),
+        out_specs=pl.BlockSpec(memory_space=smem),
         scratch_shapes=[
             vmem((1, rows), jnp.int32),
             smem(piece_extents.shape, jnp.int32),
@@ -410,7 +410,7 @@
         latent_vectors, unembedding_matrix.T, drawn_symbols.reshape(1, rows),
         piece_extents, piece_episode_lookup, episode_heats,
     )
-    return out[0, :4]
+    return out
 
 
 def solution(mesh):

time: 74.2 us -> 73.7 us (level)
    squeeze x1 -> x0, local copies, waits for them, and re-layouts: 1.19 us -> none  [on_device(): return out[0, :4]]
    unnamed x0 -> x1, local copies, waits for them, and re-layouts: none -> 1.19 us
where the time goes in v3:
time: 73.7 us; the launch traced here: 73.6 us
  Pallas kernels  72.4 us (98%)
  local copies, waits for them, and re-layouts  1.19 us (2%)
    pallas_call x1, Pallas kernels, on_device(): pl.pallas_call(kernel, out_shape=jax.ShapeDtypeStruct((4,), f32), in_spec...  72.4 us

profile of v3, /device:TPU:1, one launch (start us, length us, event | category | flops | bytes accessed | tf_op | source)
XLA Modules:
  0.0 73.6 jit_solution(7614043745524146039)
XLA Ops:
  0.0 72.4 %shard_map.64 = f32[4]{0:T(128)} custom-call(f32[96,3584]{1,0:T(8,128)} %x_hbm.1, f32[594,3584]{1,0:T(8,128)} %bitcast.2, s32[1,96]{1,0:T(1,128)} %bitcast.3, s32[1,4]{1,0:T(1,128)} %ext_hbm.1, s32[1,4]{1,0:T(1,128)} %look_hbm.1, f32[1024]{0:T(1024)} %heat_hbm.1), custom_call_target="tpu_custom_call" | custom-call | tf_op jit(solution)/shard_map/pallas_call | solution.py:381
  72.4 1.2 %copy.8 = f32[4]{0:T(128)} copy(f32[4]{0:T(128)} %shard_map.64) | data formatting | bytes 32

commit v4 on v3

--- a/solution.py
+++ b/solution.py
@@ -97,7 +97,7 @@
         )
     ]
     w_copy = pltpu.make_async_copy(wt_hbm, Wf, w_sem)
-    for copy in own + small + [w_copy]:
+    for copy in own + small:
         copy.start()
     for copy in small:
         copy.wait()
@@ -116,6 +116,7 @@
     MT[...] = jnp.zeros(MT.shape, jnp.float32)
     for copy in own:
         copy.wait()
+    w_copy.start()
     pl.semaphore_wait(barrier, 30)
 
     for sidx, s in enumerate((1, -1)):

time: 73.7 us -> 73.7 us (level)
  no operation moved by 1% of the time
where the time goes in v4:
time: 73.7 us; the launch traced here: 73.6 us
  Pallas kernels  72.4 us (98%)
  local copies, waits for them, and re-layouts  1.19 us (2%)
    pallas_call x1, Pallas kernels, on_device(): pl.pallas_call(kernel, out_shape=jax.ShapeDtypeStruct((4,), f32), in_spec...  72.4 us

profile of v4, /device:TPU:1, one launch (start us, length us, event | category | flops | bytes accessed | tf_op | source)
XLA Modules:
  0.0 73.6 jit_solution(14335583006868266865)
XLA Ops:
  0.0 72.4 %shard_map.64 = f32[4]{0:T(128)} custom-call(f32[96,3584]{1,0:T(8,128)} %x_hbm.1, f32[594,3584]{1,0:T(8,128)} %bitcast.2, s32[1,96]{1,0:T(1,128)} %bitcast.3, s32[1,4]{1,0:T(1,128)} %ext_hbm.1, s32[1,4]{1,0:T(1,128)} %look_hbm.1, f32[1024]{0:T(1024)} %heat_hbm.1), custom_call_target="tpu_custom_call" | custom-call | tf_op jit(solution)/shard_map/pallas_call | solution.py:382
  72.4 1.2 %copy.8 = f32[4]{0:T(128)} copy(f32[4]{0:T(128)} %shard_map.64) | data formatting | bytes 32
